TPU v7x, 32 devices: a whole 2x2x4 slice. The times are simulated.
32 devices in a mesh: dp: 4 (over y, x), mp: 8 (over z, core).
Axes of the slice: x: 2, y: 2, z: 4, core: 2. Of those that a mesh axis runs over, the one named last changes fastest.
Arguments:
- tokens: bfloat16 [128, 6144], P(('dp', 'mp')), may hold values from -6 to 6
- norm_gain: float32 [6144], replicated, may hold values from 0.5 to 1.5
- w_query: bfloat16 [6144, 4096], P('dp', 'mp'), as said below
- w_key: bfloat16 [6144, 4096], P('dp', 'mp'), as said below
- w_value: bfloat16 [6144, 4096], P('dp', 'mp'), may hold values from -0.078125 to 0.078125
- w_inner: bfloat16 [6144, 24576], P('dp', 'mp'), may hold values from -0.078125 to 0.078125
- bias_inner: float32 [24576], P('mp'), may hold values from -3 to 3
- w_attn_out: bfloat16 [4096, 6144], P('mp', 'dp'), may hold values from -0.09375 to 0.09375
- w_outer: bfloat16 [24576, 6144], P('mp', 'dp'), may hold values from -0.0390625 to 0.0390625
- temper: float32 [32], P('mp'), may hold values from 0.5 to 24
Outputs:
- result: bfloat16 [128, 6144], P(('dp', 'mp'))
Inputs may be any that keep to these rules, and one draw needn't show every extreme that they name: `w_query`: entries of order 6144 ** -0.5. `w_key`: entries of order 6144 ** -0.5.
All inputs are finite; a program needn't handle non-finite values.
Results may differ from a plain program's by a relative error of at most 0.023.
Values may be sent and summed in bfloat16 or wider, within the bound.
A program may use at most 128 MiB of HBM per device.

v0:
```python
import math

import jax
import jax.numpy as jnp
from jax import lax
from jax.sharding import PartitionSpec as P

HEAD = 128


def normalize(values):
    center = values - jnp.mean(values, axis=-1, keepdims=True)
    spread = jnp.mean(center * center, axis=-1, keepdims=True)
    return center * lax.rsqrt(spread + 1e-06)


def per_device(
    tokens, norm_gain, w_query, w_key, w_value, w_inner, bias_inner, w_attn_out, w_outer, temper
):
    local = tokens.astype(jnp.float32)
    normed = (normalize(local) * norm_gain).astype(jnp.bfloat16)
    image = lax.all_gather(normed, "mp", axis=0, tiled=True)
    count_rows = image.shape[0]
    width_head = w_query.shape[1]
    spread_rows = lax.all_to_all(image, "dp", split_axis=1, concat_axis=0, tiled=True)
    stacked = jnp.concatenate((w_query, w_key, w_value, w_inner), axis=1)
    projected = lax.psum_scatter(
        jnp.dot(spread_rows, stacked, preferred_element_type=jnp.float32).astype(jnp.bfloat16),
        "dp",
        scatter_dimension=0,
        tiled=True,
    ).astype(jnp.float32)
    query_sum = projected[:, :width_head]
    key_sum = projected[:, width_head : 2 * width_head]
    value_sum = projected[:, 2 * width_head : 3 * width_head]
    inner_sum = projected[:, 3 * width_head :]
    heads_dev = width_head // HEAD
    shape = (count_rows, heads_dev, HEAD)
    query_norm = normalize(
        query_sum.astype(jnp.bfloat16).astype(jnp.float32).reshape(shape)
    ).astype(jnp.bfloat16)
    key_norm = normalize(key_sum.astype(jnp.bfloat16).astype(jnp.float32).reshape(shape)).astype(
        jnp.bfloat16
    )
    values = value_sum.astype(jnp.bfloat16).reshape(shape)
    scale = temper / math.sqrt(HEAD)
    scores = jnp.einsum("qhc,khc->hqk", query_norm, key_norm, preferred_element_type=jnp.float32)
    scores = scores * scale[:, None, None]
    probs = jax.nn.softmax(scores, axis=-1).astype(jnp.bfloat16)
    mixed = jnp.einsum("hqk,khc->qhc", probs, values, preferred_element_type=jnp.float32)
    mixed = mixed.astype(jnp.bfloat16).reshape(count_rows, width_head)
    inner = inner_sum + bias_inner
    activ = jax.nn.gelu(inner, approximate=False).astype(jnp.bfloat16)
    attn_full, outer_full = (
        lax.all_gather(w_attn_out, "dp", axis=1, tiled=True),
        lax.all_gather(w_outer, "dp", axis=1, tiled=True),
    )
    attn_part = lax.psum_scatter(
        jnp.dot(mixed, attn_full, preferred_element_type=jnp.float32).astype(jnp.bfloat16),
        "mp",
        scatter_dimension=0,
        tiled=True,
    ).astype(jnp.float32)
    mlp_part = lax.psum_scatter(
        jnp.dot(activ, outer_full, preferred_element_type=jnp.float32).astype(jnp.bfloat16),
        "mp",
        scatter_dimension=0,
        tiled=True,
    ).astype(jnp.float32)
    total = attn_part + mlp_part
    return (local + total).astype(jnp.bfloat16)


def solution(mesh):
    return jax.shard_map(
        per_device,
        mesh=mesh,
        in_specs=(
            P(("dp", "mp"), None),
            P(),
            P("dp", "mp"),
            P("dp", "mp"),
            P("dp", "mp"),
            P("dp", "mp"),
            P("mp"),
            P("mp", "dp"),
            P("mp", "dp"),
            P("mp"),
        ),
        out_specs=P(("dp", "mp"), None),
        check_vma=False,
    )
```

profile of v0, /device:TPU:0, one launch (start us, length us, event | category | flops | bytes accessed | tf_op | source)
XLA Modules:
  0.0 563.7 jit_solution(12790307825521817195)
XLA Ops:
  6.5 1.0 convert_reduce_fusion
  7.5 1.0 fusion.63
  8.5 0.9 fusion.67
  9.5 16.2 %all-gather = bf16[8,4,6144]{2,1,0:T(4,128)(2,1)S(1)} all-gather(bf16[1,4,6144]{2,1,0:T(4,128)(2,1)S(1)} %fusion.67), channel_id=1, replica_groups=mesh['dp'=4,'mp'=8] {'mp'}, dimensions={0}, use_global_device_ids=true | all-gather | bytes 442368 | tf_op jit(solution)/shard_map/all_gather | solution.py:22
  25.7 0.2 all_to_all.14
  25.9 0.1 copy.32
  26.0 11.1 %all_to_all.19 = bf16[32,4,1536]{2,0,1:T(8,128)(2,1)S(1)} all-to-all(bf16[32,4,1536]{2,0,1:T(8,128)(2,1)S(1)} %copy.32), channel_id=1, replica_groups=mesh['dp'=4,'mp'=8] {'dp'}, dimensions={1} | all-to-all | bytes 786432 | tf_op jit(solution)/shard_map/all_to_all | solution.py:25
  37.2 8.7 %fusion.9 = bf16[128,4608]{1,0:T(8,128)(2,1)} fusion(bf16[128,1536]{1,0:T(8,128)(2,1)S(1)} %bitcast.20, bf16[1536,3072]{1,0:T(8,128)(2,1)} %param.15, bf16[1536,512]{1,0:T(8,128)(2,1)} %param.14, bf16[1536,512]{1,0:T(8,128)(2,1)} %param.13, bf16[1536,512]{1,0:T(8,128)(2,1)} %param.12), kind=kOutput, calls=%fused_computation.11 | convolution fusion | flops 1869152256 | bytes 15728640 | tf_op jit(solution)/shard_map/dot_general | solution.py:28
  45.8 0.0 reduce-scatter.2.cloned.1.call-update
  45.9 0.0 copy-start.1
  45.9 0.0 all-gather.4.cloned.1.call-start
  45.9 0.7 all-gather.4.cloned.1.call-update
  46.6 0.0 all-gather.6.cloned.1.call-start
  46.7 0.7 all-gather.6.cloned.1.call-update
  47.4 0.0 all-reduce.5.cloned.1.call-start
  47.4 26.8 %reduce-scatter.2.cloned.1.call-done = bf16[32,4608]{1,0:T(8,128)(2,1)} async-done(((bf16[128,4608]{1,0:T(8,128)(2,1)}), bf16[32,4608]{1,0:T(8,128)(2,1)}) %reduce-scatter.2.cloned.1.call-update) | async-done | bytes 294928 | tf_op jit(solution)/shard_map/reduce_scatter | solution.py:27
  74.3 0.8 slice_bitcast_fusion
  75.1 0.1 reduce_sum.65
  75.2 0.1 reduce_sum.67
  75.4 0.2 multiply_reduce_fusion.1
  75.6 0.2 multiply_reduce_fusion
  75.8 0.2 multiply_convert_fusion
  76.0 0.2 fusion.110
  76.2 0.2 fusion.14
  76.4 69.8 %all-gather.4.cloned.1.call-done = bf16[512,6144]{1,0:T(8,128)(2,1)} async-done(((bf16[512,1536]{1,0:T(8,128)(2,1)}), bf16[512,6144]{1,0:T(8,128)(2,1)}) %all-gather.4.cloned.1.call-update) | async-done | bytes 6291472 | tf_op jit(solution)/shard_map/all_gather | solution.py:55
  146.2 4.7 convolution_convert_fusion.1
  150.9 330.0 %all-gather.6.cloned.1.call-done = bf16[3072,6144]{1,0:T(8,128)(2,1)} async-done(((bf16[3072,1536]{1,0:T(8,128)(2,1)}), bf16[3072,6144]{1,0:T(8,128)(2,1)}) %all-gather.6.cloned.1.call-update) | async-done | bytes 37748752 | tf_op jit(solution)/shard_map/all_gather | solution.py:56
  480.9 16.6 %convolution_convert_fusion = bf16[32,6144]{1,0:T(8,128)(2,1)} fusion(bf16[3072,6144]{1,0:T(8,128)(2,1)} %all-gather.6.cloned.1.call-done, bf16[32,4608]{1,0:T(8,128)(2,1)} %reduce-scatter.2.cloned.1.call-done, f32[3072]{0:T(1024)S(1)} %copy-done.1), kind=kOutput, calls=%fused_computation.9 | convolution fusion | flops 1214742528 | bytes 38350848 | tf_op jit(solution)/shard_map/dot_general | solution.py:65
  497.5 0.0 all-reduce.5.cloned.1.call-update
  497.5 0.6 dynamic-slice
  498.8 56.7 %all-reduce.5.cloned.1.call-done = (bf16[32,6144]{1,0:T(8,128)(2,1)}, bf16[32,6144]{1,0:T(8,128)(2,1)}) async-done(((bf16[32,6144]{1,0:T(8,128)(2,1)}, bf16[32,6144]{1,0:T(8,128)(2,1)}), (bf16[32,6144]{1,0:T(8,128)(2,1)}, bf16[32,6144]{1,0:T(8,128)(2,1)})) %all-reduce.5.cloned.1.call-update) | async-done | bytes 786448
  555.5 1.6 fusion.66
  (17 shorter events, 0.1 us)
Async XLA Ops:
  6.5 67.7 %reduce-scatter.2.cloned.1.call-start = ((), (), s32[]{:S(2)}) async-start(), calls=%async_computation.2 | async-start | bytes 1474560 | tf_op jit(solution)/shard_map/reduce_scatter | solution.py:27
  45.8 1.6 copy-start.2
  45.9 435.1 %copy-start.1 = (f32[3072]{0:T(1024)S(1)}, f32[3072]{0:T(1024)}, u32[]{:S(2)}) copy-start(f32[3072]{0:T(1024)} %param.16) | copy-start | bytes 36868
  45.9 100.3 %all-gather.4.cloned.1.call-start = ((), (), s32[]{:S(2)}) async-start(), calls=%async_computation.3 | async-start | bytes 7864320 | tf_op jit(solution)/shard_map/all_gather | solution.py:55
  46.6 434.3 %all-gather.6.cloned.1.call-start = ((), (), s32[]{:S(2)}) async-start(), calls=%async_computation.4 | async-start | bytes 47185920 | tf_op jit(solution)/shard_map/all_gather | solution.py:56
  47.4 508.1 %all-reduce.5.cloned.1.call-start = ((), (), s32[]{:S(2)}) async-start(), calls=%async_computation.5 | async-start | bytes 1572864
  150.9 346.6 %copy-start.3 = (u32[32]{0:T(128)S(1)}, u32[32]{0:T(128)}, u32[]{:S(2)}) copy-start(u32[32]{0:T(128)} %constant.84) | copy-start | bytes 388
  150.9 404.6 %copy-start = (bf16[4,6144]{1,0:T(4,128)(2,1)S(1)}, bf16[4,6144]{1,0:T(4,128)(2,1)}, u32[]{:S(2)}) copy-start(bf16[4,6144]{1,0:T(4,128)(2,1)} %param.10) | copy-start | bytes 147460
Sparse Core Ops, SparseCore 0:
  46.0 28.2 reduce-scatter.1
  76.1 70.0 all-gather.3
  148.0 332.8 all-gather.5
  497.6 57.8 all-reduce.4
where the time goes:
time: 564 us
  waiting for transfers between devices  485 us (86%)
  matrix products  30.4 us (5%)
  blocking collectives  27.4 us (5%)
  between operations  13.9 us (2%)
  other arithmetic  6.14 us (1%)
    all_gather x1, waiting for transfers between devices, per_device(): lax.all_gather(w_outer, 'dp', axis=1, tiled=True)  330 us
    all_gather x1, waiting for transfers between devices, per_device(): lax.all_gather(w_attn_out, 'dp', axis=1, tiled=True)  69.8 us
    unnamed x5, waiting for transfers between devices  58.1 us
    reduce_scatter x1, waiting for transfers between devices, per_device(): lax.psum_scatter(jnp.dot(spread_rows, stacked, preferred_element_type=jnp...  26.8 us
    dot_general x1, matrix products, per_device(): jnp.dot(activ, outer_full, preferred_element_type=jnp.float32)  16.6 us
    all_gather x1, blocking collectives, per_device(): image = lax.all_gather(normed, 'mp', axis=0, tiled=True)  16.2 us
  transfers between devices with their start and end apart: 4, of which 4 were waited for; matrix products, arithmetic and copies ran while one was open for 1% of the time, Pallas kernels for 0%

commit v1 on v0

v1 whole, which is shorter than its diff:
```python
import math

import jax
import jax.numpy as jnp
from jax import lax
from jax.sharding import PartitionSpec as P

HEAD = 128


def normalize(values):
    center = values - jnp.mean(values, axis=-1, keepdims=True)
    spread = jnp.mean(center * center, axis=-1, keepdims=True)
    return center * lax.rsqrt(spread + 1e-06)


def per_device(
    tokens, norm_gain, w_query, w_key, w_value, w_inner, bias_inner, w_attn_out, w_outer, temper
):
    f32, bf16 = jnp.float32, jnp.bfloat16
    n_dp, n_mp = lax.axis_size("dp"), lax.axis_size("mp")
    local = tokens.astype(f32)
    rows = tokens.shape[0]
    normed = (normalize(local) * norm_gain).astype(bf16)
    part = lax.all_to_all(normed.reshape(rows, n_dp, -1), "dp", split_axis=1, concat_axis=0)
    part = part.reshape(n_dp, rows, -1)
    spread = lax.all_gather(part, "mp", axis=1)
    spread = spread.reshape(n_dp * n_mp * rows, -1)

    def project(weight):
        out = jnp.dot(spread, weight, preferred_element_type=f32).astype(bf16)
        return out

    width_head = w_query.shape[1]
    stacked = jnp.concatenate([project(w) for w in (w_query, w_key, w_value, w_inner)], axis=1)
    projected = lax.psum_scatter(stacked, "dp", scatter_dimension=0, tiled=True).astype(f32)
    count_rows = n_mp * rows
    heads_dev = width_head // HEAD
    shape = (count_rows, heads_dev, HEAD)
    query_norm = normalize(projected[:, :width_head].reshape(shape)).astype(bf16)
    key_norm = normalize(projected[:, width_head : 2 * width_head].reshape(shape)).astype(bf16)
    values = projected[:, 2 * width_head : 3 * width_head].astype(bf16).reshape(shape)
    scale = temper / math.sqrt(HEAD)
    scores = jnp.einsum("qhc,khc->hqk", query_norm, key_norm, preferred_element_type=f32)
    scores = scores * scale[:, None, None]
    probs = jax.nn.softmax(scores, axis=-1).astype(bf16)
    mixed = jnp.einsum("hqk,khc->qhc", probs, values, preferred_element_type=f32)
    mixed = mixed.astype(bf16).reshape(count_rows, width_head)
    inner = projected[:, 3 * width_head :] + bias_inner
    activ = jax.nn.gelu(inner, approximate=False).astype(bf16)
    hidden = lax.all_gather(jnp.concatenate((mixed, activ), axis=1), "dp", axis=0, tiled=True)
    out = jnp.dot(hidden[:, :width_head], w_attn_out, preferred_element_type=f32)
    out = out + jnp.dot(hidden[:, width_head:], w_outer, preferred_element_type=f32)
    out = out.astype(bf16).reshape(n_dp, n_mp, rows, -1)
    out = lax.psum_scatter(out, "mp", scatter_dimension=1, tiled=False)
    out = lax.all_to_all(out, "dp", split_axis=0, concat_axis=1).reshape(rows, -1)
    return (local + out.astype(f32)).astype(bf16)


def solution(mesh):
    return jax.shard_map(
        per_device,
        mesh=mesh,
        in_specs=(
            P(("dp", "mp"), None),
            P(),
            P("dp", "mp"),
            P("dp", "mp"),
            P("dp", "mp"),
            P("dp", "mp"),
            P("mp"),
            P("mp", "dp"),
            P("mp", "dp"),
            P("mp"),
        ),
        out_specs=P(("dp", "mp"), None),
        check_vma=False,
    )
```

time: 564 us -> 168 us (0.30)
  waiting for transfers between devices: 485 us -> 83.6 us
  matrix products: 30.4 us -> 12.9 us
  blocking collectives: 27.4 us -> 44.6 us
    all_gather x2 -> x0, waiting for transfers between devices: 400 us -> none  [the longest x1 330 us: per_device(): lax.all_gather(w_outer, 'dp', axis=1, tiled=True)]
    dot_general x4 -> x7, matrix products: 30.2 us -> 12.8 us  [the longest x4 6.31 us: project(): out = jnp.dot(spread, weight, preferred_element_type=f32).astype(bf16)]
    all_gather x1 -> x2, blocking collectives: 16.2 us -> 26.6 us  [the longest x1 14.7 us: per_device(): spread = lax.all_gather(part, 'mp', axis=1)]
    all_to_all x1 -> x2, blocking collectives: 11.1 us -> 18 us  [the longest x1 9.79 us: per_device(): lax.all_to_all(normed.reshape(rows, n_dp, -1), 'dp', split_axis=1, concat...]
    unnamed x5 -> x3, waiting for transfers between devices: 58.1 us -> 55.5 us
  transfers between devices with their start and end apart: 4 -> 2, of which waited for: 4 -> 2; matrix products, arithmetic and copies ran while one was open for 1% -> 0% of each run, Pallas kernels for 0% -> 0%
where the time goes in v1:
time: 168 us
  waiting for transfers between devices  83.6 us (50%)
  blocking collectives  44.6 us (27%)
  between operations  13.7 us (8%)
  matrix products  12.9 us (8%)
  other arithmetic  6.48 us (4%)
  local copies, waits for them, and re-layouts  6.11 us (4%)
    unnamed x3, waiting for transfers between devices  55.5 us
    reduce_scatter x1, waiting for transfers between devices, per_device(): lax.psum_scatter(stacked, 'dp', scatter_dimension=0, tiled=True).astype(f32)  28.1 us
    all_gather x1, blocking collectives, per_device(): spread = lax.all_gather(part, 'mp', axis=1)  14.7 us
    all_gather x1, blocking collectives, per_device(): lax.all_gather(jnp.concatenate((mixed, activ), axis=1), 'dp', axis=0, til...  11.9 us
    all_to_all x1, blocking collectives, per_device(): lax.all_to_all(normed.reshape(rows, n_dp, -1), 'dp', split_axis=1, concat...  9.79 us
    all_to_all x1, blocking collectives, per_device(): lax.all_to_all(out, 'dp', split_axis=0, concat_axis=1).reshape(rows, -1)  8.25 us
    dot_general x4, matrix products, project(): out = jnp.dot(spread, weight, preferred_element_type=f32).astype(bf16)  6.31 us
    dot_general x1, matrix products, per_device(): jnp.dot(hidden[:, width_head:], w_outer, preferred_element_type=f32)  5.1 us
  transfers between devices with their start and end apart: 2, of which 2 were waited for; matrix products, arithmetic and copies ran while one was open for 0% of the time, Pallas kernels for 0%

profile of v1, /device:TPU:0, one launch (start us, length us, event | category | flops | bytes accessed | tf_op | source)
XLA Modules:
  0.0 167.6 jit_solution(15498595041612455471)
XLA Ops:
  6.5 1.1 convert_reduce_fusion
  7.6 1.0 fusion.20
  8.7 0.9 fusion.22
  9.6 9.8 %all_to_all.24 = bf16[1,4,4,1536]{3,1,0,2:T(4,128)(2,1)S(1)} all-to-all(bf16[1,4,4,1536]{3,1,0,2:T(4,128)(2,1)S(1)} %bitcast.46), channel_id=1, replica_groups=mesh['dp'=4,'mp'=8] {'dp'}, dimensions={2} | all-to-all | bytes 98304 | tf_op jit(solution)/shard_map/all_to_all | solution.py:25
  19.4 14.7 %all-gather = bf16[4,8,4,1,1536]{4,2,3,0,1:T(4,128)(2,1)S(1)} all-gather(bf16[4,1,4,1,1536]{4,2,3,0,1:T(4,128)(2,1)S(1)} %bitcast.45), channel_id=2, replica_groups=mesh['dp'=4,'mp'=8] {'mp'}, dimensions={1}, use_global_device_ids=true | all-gather | bytes 442368 | tf_op jit(solution)/shard_map/all_gather | solution.py:27
  34.1 0.1 copy.32
  34.4 5.2 %convolution_convert_fusion = bf16[128,3072]{1,0:T(8,128)(2,1)S(1)} fusion(bf16[128,1536]{1,0:T(8,128)(2,1)S(1)} %reshape.65, bf16[1536,3072]{1,0:T(8,128)(2,1)} %param.15), kind=kOutput, calls=%fused_computation.1 | convolution fusion | flops 1208352768 | bytes 10616832 | tf_op jit(solution)/shard_map/dot_general | solution.py:31
  39.6 0.4 convolution_convert_fusion.1
  40.0 1.0 copy-done.2
  41.0 0.4 convolution_convert_fusion.2
  41.4 1.0 copy-done.3
  42.4 0.4 convolution_convert_fusion.3
  42.8 1.1 pad_maximum_fusion
  44.0 28.1 %reduce-scatter.3.cloned.1.call-done = bf16[32,4608]{1,0:T(8,128)(2,1)} async-done(((bf16[128,4608]{1,0:T(8,128)(2,1)}), bf16[32,4608]{1,0:T(8,128)(2,1)}) %reduce-scatter.3.cloned.1.call-update) | async-done | bytes 294928 | tf_op jit(solution)/shard_map/reduce_scatter | solution.py:36
  72.1 0.8 fusion.33
  73.0 0.1 reduce_sum.65
  73.1 0.2 multiply_reduce_fusion.1
  73.3 0.1 reduce_sum.67
  73.4 0.2 multiply_reduce_fusion
  73.6 0.2 multiply_convert_fusion
  73.9 0.2 fusion.34
  74.0 1.0 fusion.4
  75.1 0.9 fusion.9
  76.0 11.9 %all_gather.7 = bf16[128,3584]{1,0:T(8,128)(2,1)S(1)} all-gather(bf16[32,3584]{1,0:T(8,128)(2,1)S(1)} %pad_maximum_fusion.1), channel_id=1, replica_groups=mesh['dp'=4,'mp'=8] {'dp'}, dimensions={0}, use_global_device_ids=true | all-gather | bytes 1146880 | tf_op jit(solution)/shard_map/all_gather | solution.py:51
  87.8 5.1 %fusion.5 = f32[128,1536]{1,0:T(8,128)S(1)} fusion(bf16[3072,1536]{1,0:T(8,128)(2,1)} %param.18, bf16[128,3584]{1,0:T(8,128)(2,1)S(1)} %all_gather.7), kind=kOutput, calls=%fused_computation.13 | convolution fusion | flops 1207959552 | bytes 11010048 | tf_op jit(solution)/shard_map/dot_general | solution.py:53
  93.0 0.4 fusion.1
  93.4 0.8 reshape.70
  94.2 0.6 dynamic-slice
  94.8 55.5 %all-reduce.3.cloned.1.call-done = bf16[4,8,4,1536]{3,2,1,0:T(4,128)(2,1)} async-done(((bf16[4,8,4,1536]{3,2,1,0:T(4,128)(2,1)}), bf16[4,8,4,1536]{3,2,1,0:T(4,128)(2,1)}) %all-reduce.3.cloned.1.call-update) | async-done | bytes 393232
  150.3 1.5 dynamic-slice_bitcast_fusion
  151.8 8.2 %all_to_all.25 = bf16[4,4,1,1536]{3,1,2,0:T(4,128)(2,1)S(1)} all-to-all(bf16[4,4,1,1536]{3,1,2,0:T(4,128)(2,1)S(1)} %dynamic-slice_bitcast_fusion), channel_id=1, replica_groups=mesh['dp'=4,'mp'=8] {'dp'}, dimensions={0} | all-to-all | bytes 98304 | tf_op jit(solution)/shard_map/all_to_all | solution.py:56
  160.1 0.6 fusion.23
  (34 shorter events, 0.4 us)
Async XLA Ops:
  6.5 86.4 %copy-start = (bf16[512,1536]{1,0:T(8,128)(2,1)S(1)}, bf16[512,1536]{1,0:T(8,128)(2,1)}, u32[]{:S(2)}) copy-start(bf16[512,1536]{1,0:T(8,128)(2,1)} %param.17) | copy-start | bytes 4718596
  6.5 65.5 %reduce-scatter.3.cloned.1.call-start = ((), (), s32[]{:S(2)}) async-start(), calls=%async_computation.3 | async-start | bytes 1474560 | tf_op jit(solution)/shard_map/reduce_scatter | solution.py:36
  34.3 5.2 %copy-start.1 = (bf16[1536,512]{1,0:T(8,128)(2,1)S(1)}, bf16[1536,512]{1,0:T(8,128)(2,1)}, u32[]{:S(2)}) copy-start(bf16[1536,512]{1,0:T(8,128)(2,1)} %param.14) | copy-start | bytes 4718596
  39.6 1.4 copy-start.2
  41.0 1.4 copy-start.3
  42.8 1.2 copy-start.7
  43.9 31.2 %copy-start.6 = (f32[3072]{0:T(1024)S(1)}, f32[3072]{0:T(1024)}, u32[]{:S(2)}) copy-start(f32[3072]{0:T(1024)} %param.16) | copy-start | bytes 36868
  43.9 106.4 %all-reduce.3.cloned.1.call-start = ((), (), s32[]{:S(2)}) async-start(), calls=%async_computation.4 | async-start | bytes 786432
  72.1 2.9 %copy-start.5 = (bf16[32,4608]{1,0:T(8,128)(2,1)S(1)}, bf16[32,4608]{1,0:T(8,128)(2,1)}, u32[]{:S(2)}) copy-start(bf16[32,4608]{1,0:T(8,128)(2,1)} %reduce-scatter.3.cloned.1.call-done) | copy-start | bytes 884740
  92.9 1.3 copy-start.8
  93.0 67.1 %copy-start.4 = (bf16[4,6144]{1,0:T(4,128)(2,1)S(1)}, bf16[4,6144]{1,0:T(4,128)(2,1)}, u32[]{:S(2)}) copy-start(bf16[4,6144]{1,0:T(4,128)(2,1)} %param.10) | copy-start | bytes 147460
Sparse Core Ops, SparseCore 0:
  44.0 28.0 reduce-scatter.2
  94.4 55.9 all-reduce.2

commit v2 on v1

v2 whole, which is shorter than its diff:
```python
import functools
import math

import jax
import jax.numpy as jnp
from jax import lax
from jax.experimental import pallas as pl
from jax.experimental.pallas import tpu as pltpu
from jax.sharding import PartitionSpec as P

HEAD = 128
MESH = pl.DeviceIdType.MESH
F32, BF16 = jnp.float32, jnp.bfloat16


def normalize(values):
    center = values - jnp.mean(values, axis=-1, keepdims=True)
    spread = jnp.mean(center * center, axis=-1, keepdims=True)
    return center * lax.rsqrt(spread + 1e-06)


def wait_bytes(ref, sem):
    pltpu.make_async_copy(ref, ref, sem).wait()


def block_kernel(
    n_dp, n_mp,
    tokens, gain, bias, temper, w_query, w_key, w_value, w_inner, w_attn, w_outer,
    out,
    w_in, w_out, nsend, nrecv, stage, x, psend, precv, ag, acc, dsend, drecv,
    win_sem, wout_sem, a_send, a_recv, p_send, p_recv, g_send, g_recv, d_send, d_recv,
):
    n_dev = n_dp * n_mp
    rows = tokens.shape[0]
    n_in, depth, wide = w_in.shape
    n_out = w_out.shape[0]
    per = psend.shape[2]
    i, j = lax.axis_index("dp"), lax.axis_index("mp")
    me = i * n_mp + j

    barrier = pltpu.get_barrier_semaphore()

    def greet(d, carry):
        t = lax.rem(me + d, n_dev)
        pl.semaphore_signal(
            barrier, inc=1, device_id=(t // n_mp, lax.rem(t, n_mp)), device_id_type=MESH
        )
        return carry

    lax.fori_loop(1, n_dev, greet, 0)

    for c, w in enumerate((w_query, w_key, w_value)):
        pltpu.make_async_copy(w, w_in.at[c], win_sem.at[c]).start()
    for c in range(3, n_in):
        pltpu.make_async_copy(
            w_inner.at[:, pl.ds((c - 3) * wide, wide)], w_in.at[c], win_sem.at[c]
        ).start()
    pltpu.make_async_copy(w_attn, w_out.at[0], wout_sem.at[0]).start()
    for c in range(1, n_out):
        pltpu.make_async_copy(
            w_outer.at[pl.ds((c - 1) * wide, wide), :], w_out.at[c], wout_sem.at[c]
        ).start()

    normed = (normalize(tokens[...].astype(F32)) * gain[...]).astype(BF16)
    for p in range(n_dp):
        nsend[p] = normed[:, p * depth : (p + 1) * depth]
    nrecv[me] = nsend[i]
    pl.semaphore_wait(barrier, n_dev - 1)

    def scatter_normed(d, carry):
        t = lax.rem(me + d, n_dev)
        ti, tj = t // n_mp, lax.rem(t, n_mp)
        pltpu.make_async_remote_copy(
            src_ref=nsend.at[ti], dst_ref=nrecv.at[me], send_sem=a_send, recv_sem=a_recv,
            device_id=(ti, tj), device_id_type=MESH,
        ).start()
        return carry

    lax.fori_loop(1, n_dev, scatter_normed, 0)
    wait_bytes(nrecv.at[pl.ds(0, n_dev - 1)], a_recv)
    for s in range(n_dev):
        stage[s * rows : (s + 1) * rows, :] = nrecv[s].astype(F32)
    x[...] = stage[...].astype(BF16)

    def project(c, carry):
        pltpu.make_async_copy(w_query, w_in.at[c], win_sem.at[c]).wait()
        part = jnp.dot(x[...], w_in[c], preferred_element_type=F32).astype(BF16)
        psend[c] = part.reshape(n_dp, per, wide)
        precv[c, i] = psend[c, i]
        for d in range(1, n_dp):
            p = lax.rem(i + d, n_dp)
            pltpu.make_async_remote_copy(
                src_ref=psend.at[c, p], dst_ref=precv.at[c, i],
                send_sem=p_send, recv_sem=p_recv.at[c],
                device_id=(p, j), device_id_type=MESH,
            ).start()
        return carry

    lax.fori_loop(0, n_in, project, 0)

    def reduced(c):
        wait_bytes(precv.at[c, pl.ds(0, n_dp - 1)], p_recv.at[c])
        total = precv[c, 0].astype(F32)
        for p in range(1, n_dp):
            total = total + precv[c, p].astype(F32)
        return total

    def share(h, value):
        ag[h, i] = value
        for d in range(1, n_dp):
            p = lax.rem(i + d, n_dp)
            pltpu.make_async_remote_copy(
                src_ref=ag.at[h, i], dst_ref=ag.at[h, i],
                send_sem=g_send, recv_sem=g_recv.at[h],
                device_id=(p, j), device_id_type=MESH,
            ).start()

    query, key, value = reduced(0), reduced(1), reduced(2)
    mixed = []
    for h in range(wide // HEAD):
        cols = slice(h * HEAD, (h + 1) * HEAD)
        query_norm = normalize(query[:, cols].astype(BF16).astype(F32)).astype(BF16)
        key_norm = normalize(key[:, cols].astype(BF16).astype(F32)).astype(BF16)
        scores = lax.dot_general(
            query_norm, key_norm, (((1,), (1,)), ((), ())), preferred_element_type=F32
        )
        scores = scores * (temper[h] * (1.0 / math.sqrt(HEAD)))
        weight = jnp.exp(scores - jnp.max(scores, axis=-1, keepdims=True))
        probs = (weight / jnp.sum(weight, axis=-1, keepdims=True)).astype(BF16)
        mixed.append(
            jnp.dot(probs, value[:, cols].astype(BF16), preferred_element_type=F32).astype(BF16)
        )
    share(0, jnp.concatenate(mixed, axis=1))

    def activate(h, carry):
        at = pl.multiple_of((h - 1) * wide, HEAD)
        inner = reduced(h + 2) + bias[:, pl.ds(at, wide)]
        activ = 0.5 * inner * (1.0 + lax.erf(inner * math.sqrt(0.5)))
        share(h, activ.astype(BF16))
        return carry

    lax.fori_loop(1, n_out, activate, 0)

    acc[...] = jnp.zeros_like(acc)

    def project_out(h, carry):
        pltpu.make_async_copy(w_attn, w_out.at[h], wout_sem.at[h]).wait()
        wait_bytes(ag.at[h, pl.ds(0, n_dp - 1)], g_recv.at[h])
        acc[...] += jnp.dot(
            ag[h].reshape(n_dp * per, wide), w_out[h], preferred_element_type=F32
        )
        return carry

    lax.fori_loop(0, n_out, project_out, 0)

    for t in range(n_dev):
        dsend[t] = acc[t * rows : (t + 1) * rows, :].astype(BF16)
    drecv[me] = dsend[me]

    def scatter_out(d, carry):
        t = lax.rem(me + d, n_dev)
        pltpu.make_async_remote_copy(
            src_ref=dsend.at[t], dst_ref=drecv.at[me], send_sem=d_send, recv_sem=d_recv,
            device_id=(t // n_mp, lax.rem(t, n_mp)), device_id_type=MESH,
        ).start()
        return carry

    lax.fori_loop(1, n_dev, scatter_out, 0)
    wait_bytes(drecv.at[pl.ds(0, n_dev - 1)], d_recv)
    for p in range(n_dp):
        total = drecv[p * n_mp].astype(F32)
        for q in range(1, n_mp):
            total = total + drecv[p * n_mp + q].astype(F32)
        cols = slice(p * depth, (p + 1) * depth)
        out[:, cols] = (tokens[:, cols].astype(F32) + total).astype(BF16)

    wait_bytes(nrecv.at[pl.ds(0, n_dev - 1)], a_send)
    wait_bytes(precv.at[:, pl.ds(0, n_dp - 1)], p_send)
    wait_bytes(ag.at[:, pl.ds(0, n_dp - 1)], g_send)
    wait_bytes(drecv.at[pl.ds(0, n_dev - 1)], d_send)


def per_device(
    n_dp, n_mp,
    tokens, norm_gain, w_query, w_key, w_value, w_inner, bias_inner, w_attn_out, w_outer, temper
):
    rows, width = tokens.shape
    depth, wide = w_query.shape
    hidden = w_inner.shape[1]
    n_dev, per = n_dp * n_mp, n_mp * rows
    n_in, n_out = 3 + hidden // wide, 1 + hidden // wide
    vmem = pl.BlockSpec(memory_space=pltpu.VMEM)
    smem = pl.BlockSpec(memory_space=pltpu.SMEM)
    hbm = pl.BlockSpec(memory_space=pl.ANY)
    dma = pltpu.SemaphoreType.DMA
    return pl.pallas_call(
        functools.partial(block_kernel, n_dp, n_mp),
        out_shape=jax.ShapeDtypeStruct((rows, width), BF16),
        in_specs=[vmem, vmem, vmem, smem] + [hbm] * 6,
        out_specs=vmem,
        scratch_shapes=[
            pltpu.VMEM((n_in, depth, wide), BF16),
            pltpu.VMEM((n_out, wide, depth), BF16),
            pltpu.VMEM((n_dp, rows, depth), BF16),
            pltpu.VMEM((n_dev, rows, depth), BF16),
            pltpu.VMEM((n_dev * rows, depth), F32),
            pltpu.VMEM((n_dev * rows, depth), BF16),
            pltpu.VMEM((n_in, n_dp, per, wide), BF16),
            pltpu.VMEM((n_in, n_dp, per, wide), BF16),
            pltpu.VMEM((n_out, n_dp, per, wide), BF16),
            pltpu.VMEM((n_dev * rows, depth), F32),
            pltpu.VMEM((n_dev, rows, depth), BF16),
            pltpu.VMEM((n_dev, rows, depth), BF16),
            dma((n_in,)), dma((n_out,)), dma, dma, dma, dma((n_in,)), dma, dma((n_out,)), dma, dma,
        ],
        compiler_params=pltpu.CompilerParams(
            collective_id=0, has_side_effects=True, vmem_limit_bytes=60 * 1024 * 1024
        ),
        name="encoder_block",
    )(
        tokens, norm_gain.reshape(1, -1), bias_inner.reshape(1, -1), temper,
        w_query, w_key, w_value, w_inner, w_attn_out, w_outer,
    )


def solution(mesh):
    return jax.shard_map(
        functools.partial(per_device, mesh.shape["dp"], mesh.shape["mp"]),
        mesh=mesh,
        in_specs=(
            P(("dp", "mp"), None),
            P(),
            P("dp", "mp"),
            P("dp", "mp"),
            P("dp", "mp"),
            P("dp", "mp"),
            P("mp"),
            P("mp", "dp"),
            P("mp", "dp"),
            P("mp"),
        ),
        out_specs=P(("dp", "mp"), None),
        check_vma=False,
    )
```

time: 168 us -> 56.6 us (0.34)
  waiting for transfers between devices: 83.6 us -> 0 us
  Pallas kernels: 0 us -> 54.9 us
  blocking collectives: 44.6 us -> 0 us
  between operations: 13.7 us -> 0.01 us
  matrix products: 12.9 us -> 0 us
  other arithmetic: 6.48 us -> 0 us
  local copies, waits for them, and re-layouts: 6.11 us -> 1.44 us
    unnamed x3 -> x0, waiting for transfers between devices: 55.5 us -> none
    pallas_call x0 -> x1, Pallas kernels: none -> 54.9 us  [per_device(): pl.pallas_call(functools.partial(block_kernel, n_dp, n_mp), out_shape=jax...]
    reduce_scatter x1 -> x0, waiting for transfers between devices: 28.1 us -> none  [per_device(): lax.psum_scatter(stacked, 'dp', scatter_dimension=0, tiled=True).astype(f32)]
    all_gather x2 -> x0, blocking collectives: 26.6 us -> none  [the longest x1 14.7 us: per_device(): spread = lax.all_gather(part, 'mp', axis=1)]
    all_to_all x2 -> x0, blocking collectives: 18 us -> none  [the longest x1 9.79 us: per_device(): lax.all_to_all(normed.reshape(rows, n_dp, -1), 'dp', split_axis=1, concat...]
    dot_general x7 -> x0, matrix products: 12.8 us -> none  [the longest x4 6.31 us: project(): out = jnp.dot(spread, weight, preferred_element_type=f32).astype(bf16)]
    reduce_sum x6 -> x0, other arithmetic: 2.68 us -> none  [the longest x3 1.39 us: normalize(): spread = jnp.mean(center * center, axis=-1, keepdims=True)]
    convert_element_type x6 -> x0, other arithmetic: 2.66 us -> none  [the longest x1 0.9 us: per_device(): normed = (normalize(local) * norm_gain).astype(bf16)]
  transfers between devices with their start and end apart: 2 -> 0, of which waited for: 2 -> 0; matrix products, arithmetic and copies ran while one was open for 0% -> 0% of each run, Pallas kernels for 0% -> 0%
where the time goes in v2:
time: 56.6 us; the launch traced here: 56.4 us
  Pallas kernels  54.9 us (97%)
  local copies, waits for them, and re-layouts  1.44 us (3%)
    pallas_call x1, Pallas kernels, per_device(): pl.pallas_call(functools.partial(block_kernel, n_dp, n_mp), out_shape=jax...  54.9 us
    unnamed x1, local copies, waits for them, and re-layouts  1.44 us

profile of v2, /device:TPU:0, one launch (start us, length us, event | category | flops | bytes accessed | tf_op | source)
XLA Modules:
  0.0 56.4 jit_solution(15216499125991656995)
XLA Ops:
  0.0 54.9 %encoder_block.1 = bf16[4,6144]{1,0:T(4,128)(2,1)} custom-call(bf16[4,6144]{1,0:T(4,128)(2,1)} %tokens.1, f32[1,6144]{1,0:T(1,128)} %bitcast.2, f32[1,3072]{1,0:T(1,128)} %bitcast.3, f32[4]{0:T(128)} %temper.1, bf16[1536,512]{1,0:T(8,128)(2,1)} %w_query.1, bf16[1536,512]{1,0:T(8,128)(2,1)} %w_key.1, bf16[1536,512]{1,0:T(8,128)(2,1)} %w_value.1, ...), custom_call_target="tpu_custom_call" | custom-call | tf_op jit(solution)/shard_map/encoder_block/pallas_call | solution.py:196
  54.9 1.4 %copy.12 = bf16[4,6144]{1,0:T(4,128)(2,1)} copy(bf16[4,6144]{1,0:T(4,128)(2,1)} %encoder_block.1) | data formatting | bytes 98304

commit v3 on v2

--- a/solution.py
+++ b/solution.py
@@ -27,8 +27,9 @@
     n_dp, n_mp,
     tokens, gain, bias, temper, w_query, w_key, w_value, w_inner, w_attn, w_outer,
     out,
-    w_in, w_out, nsend, nrecv, stage, x, psend, precv, ag, acc, dsend, drecv,
-    win_sem, wout_sem, a_send, a_recv, p_send, p_recv, g_send, g_recv, d_send, d_recv,
+    w_in, w_out, nsend, nrecv, stage, x, psend, precv, ag, acc, xsend, xrecv, dsend, drecv,
+    win_sem, wout_sem, a_send, a_recv, f_send, f_recv, p_send, p_recv, g_send, g_recv,
+    x_send, x_recv, d_send, d_recv,
 ):
     n_dev = n_dp * n_mp
     rows = tokens.shape[0]
@@ -37,6 +38,14 @@
     per = psend.shape[2]
     i, j = lax.axis_index("dp"), lax.axis_index("mp")
     me = i * n_mp + j
+    n_chip = n_mp // 2
+    n_lane = n_dp * n_chip
+    core, chip = lax.rem(j, 2), j // 2
+    sibling = (i, j + 1 - 2 * core)
+    lane = i * n_chip + chip
+
+    def same_core(other):
+        return (other // n_chip, 2 * lax.rem(other, n_chip) + core)
 
     barrier = pltpu.get_barrier_semaphore()
 
@@ -68,16 +77,31 @@
     pl.semaphore_wait(barrier, n_dev - 1)
 
     def scatter_normed(d, carry):
-        t = lax.rem(me + d, n_dev)
-        ti, tj = t // n_mp, lax.rem(t, n_mp)
+        target = same_core(lax.rem(lane + d, n_lane))
         pltpu.make_async_remote_copy(
-            src_ref=nsend.at[ti], dst_ref=nrecv.at[me], send_sem=a_send, recv_sem=a_recv,
-            device_id=(ti, tj), device_id_type=MESH,
-        ).start()
-        return carry
-
-    lax.fori_loop(1, n_dev, scatter_normed, 0)
-    wait_bytes(nrecv.at[pl.ds(0, n_dev - 1)], a_recv)
+            src_ref=nsend.at[target[0]], dst_ref=nrecv.at[me],
+            send_sem=a_send, recv_sem=a_recv.at[d],
+            device_id=target, device_id_type=MESH,
+        ).start()
+        return carry
+
+    def pass_on(source):
+        pltpu.make_async_remote_copy(
+            src_ref=nrecv.at[source], dst_ref=nrecv.at[source], send_sem=f_send, recv_sem=f_recv,
+            device_id=sibling, device_id_type=MESH,
+        ).start()
+
+    lax.fori_loop(1, n_lane, scatter_normed, 0)
+    pass_on(me)
+
+    def forward_normed(d, carry):
+        wait_bytes(nrecv.at[0], a_recv.at[d])
+        source = same_core(lax.rem(lane + n_lane - d, n_lane))
+        pass_on(source[0] * n_mp + source[1])
+        return carry
+
+    lax.fori_loop(1, n_lane, forward_normed, 0)
+    wait_bytes(nrecv.at[pl.ds(0, n_lane)], f_recv)
     for s in range(n_dev):
         stage[s * rows : (s + 1) * rows, :] = nrecv[s].astype(F32)
     x[...] = stage[...].astype(BF16)
@@ -148,36 +172,55 @@
         wait_bytes(ag.at[h, pl.ds(0, n_dp - 1)], g_recv.at[h])
         acc[...] += jnp.dot(
             ag[h].reshape(n_dp * per, wide), w_out[h], preferred_element_type=F32
-        )
+        ).reshape(acc.shape)
         return carry
 
     lax.fori_loop(0, n_out, project_out, 0)
 
-    for t in range(n_dev):
-        dsend[t] = acc[t * rows : (t + 1) * rows, :].astype(BF16)
-    drecv[me] = dsend[me]
-
-    def scatter_out(d, carry):
-        t = lax.rem(me + d, n_dev)
+    def halves(p, q):
+        tile = acc[p, 2 * rows * q : 2 * rows * (q + 1), :]
+        low, high = tile[:rows], tile[rows:]
+        return jnp.where(core == 0, low, high), jnp.where(core == 0, high, low)
+
+    for k in range(n_dp):
+        p = lax.rem(i + 1 + k, n_dp)
+        for q in range(n_chip):
+            xsend[p, q] = halves(p, q)[1].astype(BF16)
         pltpu.make_async_remote_copy(
-            src_ref=dsend.at[t], dst_ref=drecv.at[me], send_sem=d_send, recv_sem=d_recv,
-            device_id=(t // n_mp, lax.rem(t, n_mp)), device_id_type=MESH,
-        ).start()
-        return carry
-
-    lax.fori_loop(1, n_dev, scatter_out, 0)
-    wait_bytes(drecv.at[pl.ds(0, n_dev - 1)], d_recv)
+            src_ref=xsend.at[p], dst_ref=xrecv.at[p], send_sem=x_send, recv_sem=x_recv.at[k],
+            device_id=sibling, device_id_type=MESH,
+        ).start()
+
+    for k in range(n_dp):
+        p = lax.rem(i + 1 + k, n_dp)
+        wait_bytes(xrecv.at[p], x_recv.at[k])
+        for q in range(n_chip):
+            dsend[p, q] = (halves(p, q)[0] + xrecv[p, q].astype(F32)).astype(BF16)
+
+        def scatter_out(d, carry):
+            q = lax.rem(chip + d, n_chip)
+            pltpu.make_async_remote_copy(
+                src_ref=dsend.at[p, q], dst_ref=drecv.at[lane], send_sem=d_send, recv_sem=d_recv,
+                device_id=(p, 2 * q + core), device_id_type=MESH,
+            ).start()
+            return carry
+
+        lax.fori_loop(1, n_chip if k == n_dp - 1 else n_chip + 1, scatter_out, 0)
+    drecv[lane] = dsend[i, chip]
+    wait_bytes(drecv.at[pl.ds(0, n_lane - 1)], d_recv)
     for p in range(n_dp):
-        total = drecv[p * n_mp].astype(F32)
-        for q in range(1, n_mp):
-            total = total + drecv[p * n_mp + q].astype(F32)
+        total = drecv[p * n_chip].astype(F32)
+        for q in range(1, n_chip):
+            total = total + drecv[p * n_chip + q].astype(F32)
         cols = slice(p * depth, (p + 1) * depth)
         out[:, cols] = (tokens[:, cols].astype(F32) + total).astype(BF16)
 
-    wait_bytes(nrecv.at[pl.ds(0, n_dev - 1)], a_send)
+    wait_bytes(nrecv.at[pl.ds(0, n_lane - 1)], a_send)
+    wait_bytes(nrecv.at[pl.ds(0, n_lane)], f_send)
     wait_bytes(precv.at[:, pl.ds(0, n_dp - 1)], p_send)
     wait_bytes(ag.at[:, pl.ds(0, n_dp - 1)], g_send)
-    wait_bytes(drecv.at[pl.ds(0, n_dev - 1)], d_send)
+    wait_bytes(xrecv, x_send)
+    wait_bytes(drecv.at[pl.ds(0, n_lane - 1)], d_send)
 
 
 def per_device(
@@ -208,10 +251,13 @@
             pltpu.VMEM((n_in, n_dp, per, wide), BF16),
             pltpu.VMEM((n_in, n_dp, per, wide), BF16),
             pltpu.VMEM((n_out, n_dp, per, wide), BF16),
-            pltpu.VMEM((n_dev * rows, depth), F32),
-            pltpu.VMEM((n_dev, rows, depth), BF16),
-            pltpu.VMEM((n_dev, rows, depth), BF16),
-            dma((n_in,)), dma((n_out,)), dma, dma, dma, dma((n_in,)), dma, dma((n_out,)), dma, dma,
+            pltpu.VMEM((n_dp, per, depth), F32),
+            pltpu.VMEM((n_dp, n_mp // 2, rows, depth), BF16),
+            pltpu.VMEM((n_dp, n_mp // 2, rows, depth), BF16),
+            pltpu.VMEM((n_dp, n_mp // 2, rows, depth), BF16),
+            pltpu.VMEM((n_dev // 2, rows, depth), BF16),
+            dma((n_in,)), dma((n_out,)), dma, dma((n_dev // 2,)), dma, dma, dma, dma((n_in,)),
+            dma, dma((n_out,)), dma, dma((n_dp,)), dma, dma,
         ],
         compiler_params=pltpu.CompilerParams(
             collective_id=0, has_side_effects=True, vmem_limit_bytes=60 * 1024 * 1024

time: 56.6 us -> 50.3 us (0.89)
  Pallas kernels: 54.9 us -> 48.6 us
    pallas_call x1, Pallas kernels: 54.9 us -> 48.6 us  [per_device(): pl.pallas_call(functools.partial(block_kernel, n_dp, n_mp), out_shape=jax...]
where the time goes in v3:
time: 50.3 us; the launch traced here: 50.1 us
  Pallas kernels  48.6 us (97%)
  local copies, waits for them, and re-layouts  1.44 us (3%)
    pallas_call x1, Pallas kernels, per_device(): pl.pallas_call(functools.partial(block_kernel, n_dp, n_mp), out_shape=jax...  48.6 us
    unnamed x1, local copies, waits for them, and re-layouts  1.44 us

profile of v3, /device:TPU:0, one launch (start us, length us, event | category | flops | bytes accessed | tf_op | source)
XLA Modules:
  0.0 50.1 jit_solution(9894215047280925253)
XLA Ops:
  0.0 48.6 %encoder_block.1 = bf16[4,6144]{1,0:T(4,128)(2,1)} custom-call(bf16[4,6144]{1,0:T(4,128)(2,1)} %tokens.1, f32[1,6144]{1,0:T(1,128)} %bitcast.2, f32[1,3072]{1,0:T(1,128)} %bitcast.3, f32[4]{0:T(128)} %temper.1, bf16[1536,512]{1,0:T(8,128)(2,1)} %w_query.1, bf16[1536,512]{1,0:T(8,128)(2,1)} %w_key.1, bf16[1536,512]{1,0:T(8,128)(2,1)} %w_value.1, ...), custom_call_target="tpu_custom_call" | custom-call | tf_op jit(solution)/shard_map/encoder_block/pallas_call | solution.py:239
  48.7 1.4 %copy.12 = bf16[4,6144]{1,0:T(4,128)(2,1)} copy(bf16[4,6144]{1,0:T(4,128)(2,1)} %encoder_block.1) | data formatting | bytes 98304

commit v4 on v3

--- a/solution.py
+++ b/solution.py
@@ -9,6 +9,8 @@
 from jax.sharding import PartitionSpec as P
 
 HEAD = 128
+LAG_SUM = 5
+LAG_PASS = 7
 MESH = pl.DeviceIdType.MESH
 F32, BF16 = jnp.float32, jnp.bfloat16
 
@@ -106,24 +108,54 @@
         stage[s * rows : (s + 1) * rows, :] = nrecv[s].astype(F32)
     x[...] = stage[...].astype(BF16)
 
+    square = n_dp == 4
+
+    def around(c):
+        beside = i + 1 - 2 * lax.rem(i, 2)
+        across = lax.rem(i + 2, n_dp)
+        turn = lax.rem(c, 2)
+        return beside + turn * (across - beside), across + turn * (beside - across)
+
+    def send(source, target, send_sem, recv_sem, p):
+        pltpu.make_async_remote_copy(
+            src_ref=source, dst_ref=target, send_sem=send_sem, recv_sem=recv_sem,
+            device_id=(p, j), device_id_type=MESH,
+        ).start()
+
     def project(c, carry):
         pltpu.make_async_copy(w_query, w_in.at[c], win_sem.at[c]).wait()
         part = jnp.dot(x[...], w_in[c], preferred_element_type=F32).astype(BF16)
         psend[c] = part.reshape(n_dp, per, wide)
-        precv[c, i] = psend[c, i]
-        for d in range(1, n_dp):
-            p = lax.rem(i + d, n_dp)
-            pltpu.make_async_remote_copy(
-                src_ref=psend.at[c, p], dst_ref=precv.at[c, i],
-                send_sem=p_send, recv_sem=p_recv.at[c],
-                device_id=(p, j), device_id_type=MESH,
-            ).start()
-        return carry
+        if square:
+            first, _ = around(c)
+            send(psend.at[c, 3 - i], precv.at[c, 1], p_send, p_recv.at[c, 1], first)
+            send(psend.at[c, first], precv.at[c, 0], p_send, p_recv.at[c, 0], first)
+            pl.when(c >= LAG_SUM)(lambda: add_and_send(c - LAG_SUM))
+        else:
+            precv[c, i] = psend[c, i]
+            for d in range(1, n_dp):
+                p = lax.rem(i + d, n_dp)
+                send(psend.at[c, p], precv.at[c, i], p_send, p_recv.at[c, 0], p)
+        return carry
+
+    def add_and_send(c):
+        _, second = around(c)
+        wait_bytes(precv.at[c, 1], p_recv.at[c, 1])
+        precv[c, 3] = (psend[c, second].astype(F32) + precv[c, 1].astype(F32)).astype(BF16)
+        send(precv.at[c, 3], precv.at[c, 2], p_send, p_recv.at[c, 2], second)
 
     lax.fori_loop(0, n_in, project, 0)
+    if square:
+        for c in range(max(n_in - LAG_SUM, 0), n_in):
+            add_and_send(c)
 
     def reduced(c):
-        wait_bytes(precv.at[c, pl.ds(0, n_dp - 1)], p_recv.at[c])
+        if square:
+            wait_bytes(precv.at[c, 0], p_recv.at[c, 0])
+            wait_bytes(precv.at[c, 2], p_recv.at[c, 2])
+            total = psend[c, i].astype(F32) + precv[c, 0].astype(F32)
+            return total + precv[c, 2].astype(F32)
+        wait_bytes(precv.at[c, pl.ds(0, n_dp - 1)], p_recv.at[c, 0])
         total = precv[c, 0].astype(F32)
         for p in range(1, n_dp):
             total = total + precv[c, p].astype(F32)
@@ -131,13 +163,20 @@
 
     def share(h, value):
         ag[h, i] = value
-        for d in range(1, n_dp):
-            p = lax.rem(i + d, n_dp)
-            pltpu.make_async_remote_copy(
-                src_ref=ag.at[h, i], dst_ref=ag.at[h, i],
-                send_sem=g_send, recv_sem=g_recv.at[h],
-                device_id=(p, j), device_id_type=MESH,
-            ).start()
+        own = ag.at[h, i]
+        if square:
+            first, second = around(h)
+            send(own, own, g_send, g_recv.at[h, 0], second)
+            send(own, own, g_send, g_recv.at[h, 1], first)
+        else:
+            for d in range(1, n_dp):
+                send(own, own, g_send, g_recv.at[h, 0], lax.rem(i + d, n_dp))
+
+    def hand_over(h):
+        first, second = around(h)
+        block = ag.at[h, second]
+        wait_bytes(block, g_recv.at[h, 0])
+        send(block, block, g_send, g_recv.at[h, 2], first)
 
     query, key, value = reduced(0), reduced(1), reduced(2)
     mixed = []
@@ -161,15 +200,24 @@
         inner = reduced(h + 2) + bias[:, pl.ds(at, wide)]
         activ = 0.5 * inner * (1.0 + lax.erf(inner * math.sqrt(0.5)))
         share(h, activ.astype(BF16))
+        if square:
+            pl.when(h >= LAG_PASS)(lambda: hand_over(h - LAG_PASS))
         return carry
 
     lax.fori_loop(1, n_out, activate, 0)
+    if square:
+        for h in range(max(n_out - LAG_PASS, 0), n_out):
+            hand_over(h)
 
     acc[...] = jnp.zeros_like(acc)
 
     def project_out(h, carry):
         pltpu.make_async_copy(w_attn, w_out.at[h], wout_sem.at[h]).wait()
-        wait_bytes(ag.at[h, pl.ds(0, n_dp - 1)], g_recv.at[h])
+        if square:
+            wait_bytes(ag.at[h, 0], g_recv.at[h, 1])
+            wait_bytes(ag.at[h, 0], g_recv.at[h, 2])
+        else:
+            wait_bytes(ag.at[h, pl.ds(0, n_dp - 1)], g_recv.at[h, 0])
         acc[...] += jnp.dot(
             ag[h].reshape(n_dp * per, wide), w_out[h], preferred_element_type=F32
         ).reshape(acc.shape)
@@ -256,8 +304,8 @@
             pltpu.VMEM((n_dp, n_mp // 2, rows, depth), BF16),
             pltpu.VMEM((n_dp, n_mp // 2, rows, depth), BF16),
             pltpu.VMEM((n_dev // 2, rows, depth), BF16),
-            dma((n_in,)), dma((n_out,)), dma, dma((n_dev // 2,)), dma, dma, dma, dma((n_in,)),
-            dma, dma((n_out,)), dma, dma((n_dp,)), dma, dma,
+            dma((n_in,)), dma((n_out,)), dma, dma((n_dev // 2,)), dma, dma, dma, dma((n_in, 3)),
+            dma, dma((n_out, 3)), dma, dma((n_dp,)), dma, dma,
         ],
         compiler_params=pltpu.CompilerParams(
             collective_id=0, has_side_effects=True, vmem_limit_bytes=60 * 1024 * 1024

time: 50.3 us -> 47 us (0.934)
  Pallas kernels: 48.6 us -> 45.4 us
    pallas_call x1, Pallas kernels: 48.6 us -> 45.4 us  [per_device(): pl.pallas_call(functools.partial(block_kernel, n_dp, n_mp), out_shape=jax...]
where the time goes in v4:
time: 47 us; the launch traced here: 46.8 us
  Pallas kernels  45.4 us (97%)
  local copies, waits for them, and re-layouts  1.44 us (3%)
    pallas_call x1, Pallas kernels, per_device(): pl.pallas_call(functools.partial(block_kernel, n_dp, n_mp), out_shape=jax...  45.4 us
    unnamed x1, local copies, waits for them, and re-layouts  1.44 us

profile of v4, /device:TPU:0, one launch (start us, length us, event | category | flops | bytes accessed | tf_op | source)
XLA Modules:
  0.0 46.8 jit_solution(9344308323614493907)
XLA Ops:
  0.0 45.4 %encoder_block.1 = bf16[4,6144]{1,0:T(4,128)(2,1)} custom-call(bf16[4,6144]{1,0:T(4,128)(2,1)} %tokens.1, f32[1,6144]{1,0:T(1,128)} %bitcast.2, f32[1,3072]{1,0:T(1,128)} %bitcast.3, f32[4]{0:T(128)} %temper.1, bf16[1536,512]{1,0:T(8,128)(2,1)} %w_query.1, bf16[1536,512]{1,0:T(8,128)(2,1)} %w_key.1, bf16[1536,512]{1,0:T(8,128)(2,1)} %w_value.1, ...), custom_call_target="tpu_custom_call" | custom-call | tf_op jit(solution)/shard_map/encoder_block/pallas_call | solution.py:287
  45.4 1.4 %copy.12 = bf16[4,6144]{1,0:T(4,128)(2,1)} copy(bf16[4,6144]{1,0:T(4,128)(2,1)} %encoder_block.1) | data formatting | bytes 98304
